TPU v7x, 32 devices: a whole 2x2x4 slice. The times are simulated.
32 devices in a mesh: dp: 8 (over z, y), tp: 4 (over x, core).
Axes of the slice: x: 2, y: 2, z: 4, core: 2. Of those that a mesh axis runs over, the one named last changes fastest.
Arguments:
- q_latent: bfloat16 [1024, 4, 1536], P('dp'), may hold values from -6 to 6
- new_latent: bfloat16 [1024, 4, 512], P('dp'), may hold values from -6 to 6
- new_rope: bfloat16 [1024, 4, 64], P('dp'), may hold values from -6 to 6
- cache_latent: bfloat16 [1024, 256, 512], P('dp'), may hold values from -6 to 6
- cache_rope: bfloat16 [1024, 64, 256], P('dp'), may hold values from -1200 to 1200
- lengths: int32 [1024], P('dp'), may hold values from 1 to 256
- assignment: int32 [8, 128], P('dp'), may hold values from 0 to 127, each once within a row
- w_uq: float32 [1536, 12288], P(('dp', 'tp')), may hold values from -0.15625 to 0.15625
- w_uk: float32 [512, 8192], P(('dp', 'tp')), may hold values from -0.75 to 0.75
- w_uv: float32 [512, 8192], P(('dp', 'tp')), may hold values from -0.25 to 0.25
- w_o: float32 [8192, 7168], P(None, ('dp', 'tp')), may hold values from -0.0625 to 0.0625
Outputs:
- attention_out: bfloat16 [1024, 4, 7168], P('dp', None, 'tp')
- weight_norm: float32 [1], replicated
Inputs may be any that keep to these rules, and one draw needn't show every extreme that they name: Each row of assignment is a permutation of 0 to 127.
All inputs are finite; a program needn't handle non-finite values.
Results may differ from a plain program's by a relative error of at most 0.006.
The roundings to bfloat16 on the way count: a program that leaves them out, or rounds other values in their place, can miss the bound.
Values may be sent and summed in bfloat16 or wider, within the bound.
A program may use at most 256 MiB of HBM per device.

v0:
```python
import jax
import jax.numpy as jnp
from jax import lax
from jax.sharding import PartitionSpec as P

D = 7168
QRANK = 1536
KVRANK = 512
NOPE = 128
ROPE = 64
VDIM = 128
HEADS = 64
NEWTOK = 4
CACHE = 256


def widen(values):
    return lax.optimization_barrier(values).astype(jnp.float32)


def rotate_half(values, positions):
    half_width = values.shape[-1] // 2
    frequency = 10000.0 ** (-jnp.arange(half_width, dtype=jnp.float32) / half_width)
    angles = positions.astype(jnp.float32)[:, :, None, None] * frequency
    cosine = jnp.cos(angles)
    sine_part = jnp.sin(angles)
    lower_half = values[..., :half_width]
    upper_half = values[..., half_width:]
    return jnp.concatenate(
        [
            lower_half * cosine - upper_half * sine_part,
            upper_half * cosine + lower_half * sine_part,
        ],
        axis=-1,
    )


def shards(
    q_latent,
    new_latent,
    new_rope,
    cache_latent,
    cache_rope,
    lengths,
    assignment,
    w_uq,
    w_uk,
    w_uv,
    w_o,
):
    local_squares = (
        jnp.sum(w_uq * w_uq) + jnp.sum(w_uk * w_uk) + jnp.sum(w_uv * w_uv) + jnp.sum(w_o * w_o)
    )
    squares_total = lax.psum(local_squares, ("dp", "tp"))
    weight_norm = jnp.sqrt(squares_total / (HEADS * (NOPE + ROPE) + 2 * HEADS * NOPE + D)).reshape(
        1
    )
    query_cast = w_uq.astype(jnp.bfloat16)
    key_cast = w_uk.astype(jnp.bfloat16)
    value_cast = w_uv.astype(jnp.bfloat16)
    gathered = (
        lax.all_gather(query_cast[None], "dp", axis=0, tiled=True),
        lax.all_gather(key_cast[None], "dp", axis=0, tiled=True),
        lax.all_gather(value_cast[None], "dp", axis=0, tiled=True),
    )
    mixed = (
        lax.all_to_all(gathered[0], "tp", split_axis=2, concat_axis=1, tiled=True),
        lax.all_to_all(gathered[1], "tp", split_axis=2, concat_axis=1, tiled=True),
        lax.all_to_all(gathered[2], "tp", split_axis=2, concat_axis=1, tiled=True),
    )
    query_up = mixed[0].reshape(-1, mixed[0].shape[2])
    key_up = mixed[1].reshape(-1, mixed[1].shape[2])
    value_up = mixed[2].reshape(-1, mixed[2].shape[2])
    out_cast = w_o.astype(jnp.bfloat16)
    seq_count = q_latent.shape[0]
    heads_here = key_up.shape[1] // NOPE
    selector = (assignment[0][:, None] == jnp.arange(seq_count, dtype=jnp.int32)[None, :]).astype(
        jnp.bfloat16
    )

    def to_slots(array):
        moved = jnp.dot(
            selector.T, array.reshape(seq_count, -1), preferred_element_type=jnp.float32
        )
        return moved.astype(jnp.bfloat16).reshape(array.shape)

    query_slots = to_slots(q_latent)
    latent_slots = to_slots(new_latent)
    rope_slots = to_slots(new_rope)
    projected = jnp.dot(
        query_slots.reshape(seq_count * NEWTOK, QRANK), query_up, preferred_element_type=jnp.float32
    )
    projected = projected.astype(jnp.bfloat16).reshape(seq_count, NEWTOK, heads_here, NOPE + ROPE)
    query_nope = projected[..., :NOPE]
    positions = lengths[:, None] + jnp.arange(NEWTOK, dtype=jnp.int32)[None, :]
    query_rot = rotate_half(widen(projected[..., NOPE:]), positions).astype(jnp.bfloat16)
    absorbed = jnp.einsum(
        "sqhn,chn->sqhc",
        query_nope,
        key_up.reshape(KVRANK, heads_here, NOPE),
        preferred_element_type=jnp.float32,
    ).astype(jnp.bfloat16)
    scale = (NOPE + ROPE) ** (-0.5)
    cache_scores = jnp.einsum(
        "sqhc,stc->sqht", absorbed, cache_latent, preferred_element_type=jnp.float32
    )
    cache_scores = (
        cache_scores
        + jnp.einsum("sqhr,srt->sqht", query_rot, cache_rope, preferred_element_type=jnp.float32)
    ) * scale
    valid = jnp.arange(CACHE, dtype=jnp.int32)[None, :] < lengths[:, None]
    cache_scores = jnp.where(valid[:, None, None, :], cache_scores, -jnp.inf)
    new_scores = jnp.einsum(
        "sqhc,skc->sqhk", absorbed, latent_slots, preferred_element_type=jnp.float32
    )
    new_scores = (
        new_scores
        + jnp.einsum("sqhr,skr->sqhk", query_rot, rope_slots, preferred_element_type=jnp.float32)
    ) * scale
    causal = jnp.arange(NEWTOK)[:, None] >= jnp.arange(NEWTOK)[None, :]
    new_scores = jnp.where(causal[None, :, None, :], new_scores, -jnp.inf)
    scores = jnp.concatenate([cache_scores, new_scores], axis=-1)
    largest = jnp.max(scores, axis=-1, keepdims=True)
    expo = jnp.exp(scores - largest)
    weights = (expo / jnp.sum(expo, axis=-1, keepdims=True)).astype(jnp.bfloat16)
    latent_out = jnp.einsum(
        "sqht,stc->sqhc", weights[..., :CACHE], cache_latent, preferred_element_type=jnp.float32
    )
    latent_out = (
        latent_out
        + jnp.einsum(
            "sqhk,skc->sqhc", weights[..., CACHE:], latent_slots, preferred_element_type=jnp.float32
        )
    ).astype(jnp.bfloat16)
    head_out = jnp.einsum(
        "sqhc,chv->sqhv",
        latent_out,
        value_up.reshape(KVRANK, heads_here, VDIM),
        preferred_element_type=jnp.float32,
    ).astype(jnp.bfloat16)
    request_out = jnp.dot(
        selector, head_out.reshape(seq_count, -1), preferred_element_type=jnp.float32
    )
    request_out = request_out.astype(jnp.bfloat16).reshape(seq_count * NEWTOK, heads_here * VDIM)
    out_rows = lax.all_to_all(out_cast, "tp", split_axis=0, concat_axis=1, tiled=True)
    partial_out = jnp.dot(
        request_out,
        lax.all_gather(out_rows, "dp", axis=1, tiled=True),
        preferred_element_type=jnp.float32,
    )
    reduced = lax.psum_scatter(partial_out, "tp", scatter_dimension=1, tiled=True)
    attention_out = reduced.astype(jnp.bfloat16).reshape(seq_count, NEWTOK, -1)
    return (attention_out, weight_norm)


def solution(mesh):
    in_specs = (
        P("dp", None, None),
        P("dp", None, None),
        P("dp", None, None),
        P("dp", None, None),
        P("dp", None, None),
        P("dp"),
        P("dp", None),
        P(("dp", "tp"), None),
        P(("dp", "tp"), None),
        P(("dp", "tp"), None),
        P(None, ("dp", "tp")),
    )
    out_specs = (P("dp", None, "tp"), P())
    return jax.shard_map(shards, mesh=mesh, in_specs=in_specs, out_specs=out_specs, check_vma=False)
```

profile of v0, /device:TPU:0, one launch (start us, length us, event | category | flops | bytes accessed | tf_op | source)
XLA Modules:
  0.0 955.4 jit_solution(7704429652962988391)
XLA Ops:
  25.6 46.7 %all_to_all.64 = bf16[4,2048,224]{1,2,0:T(8,128)(2,1)} all-to-all(bf16[4,2048,224]{1,2,0:T(8,128)(2,1)S(1)} %bitcast.89), channel_id=1, replica_groups=mesh['dp'=8,'tp'=4] {'tp'}, dimensions={0} | all-to-all | bytes 7340032 | tf_op jit(solution)/shard_map/all_to_all | solution.py:145
  72.3 14.4 %copy.71 = bf16[8,16,8192]{1,0,2:T(8,128)(2,1)} copy(bf16[8,16,8192]{2,1,0:T(8,128)(2,1)} %bitcast.100) | data formatting | bytes 4194304 | tf_op jit(solution)/shard_map/all_gather | solution.py:63
  86.7 20.3 %reshape.140 = bf16[4,2,131072]{2,1,0:T(2,128)(2,1)} reshape(bf16[8192,8,16]{2,1,0:T(8,128)(2,1)} %bitcast.83) | data formatting | bytes 4194304
  111.8 14.4 %copy.82 = bf16[8,16,8192]{1,0,2:T(8,128)(2,1)} copy(bf16[8,16,8192]{2,1,0:T(8,128)(2,1)} %bitcast.101) | data formatting | bytes 4194304 | tf_op jit(solution)/shard_map/all_gather | solution.py:64
  126.2 20.3 %reshape.136 = bf16[4,2,131072]{2,1,0:T(2,128)(2,1)} reshape(bf16[8192,8,16]{2,1,0:T(8,128)(2,1)} %bitcast.84) | data formatting | bytes 4194304
  151.0 99.3 %all-gather.10.cloned.1.call-done = bf16[384,12288]{1,0:T(8,128)(2,1)} async-done(((bf16[48,12288]{1,0:T(8,128)(2,1)}), bf16[384,12288]{1,0:T(8,128)(2,1)}) %all-gather.10.cloned.1.call-update) | async-done | bytes 9437200 | tf_op jit(solution)/shard_map/all_gather | solution.py:62
  250.3 26.1 %copy.67 = bf16[8,48,12288]{1,0,2:T(8,128)(2,1)} copy(bf16[8,48,12288]{2,1,0:T(8,128)(2,1)} %bitcast.92) | data formatting | bytes 18874368 | tf_op jit(solution)/shard_map/all_gather | solution.py:62
  276.4 54.9 %reshape.138 = bf16[4,2,589824]{2,1,0:T(2,128)(2,1)} reshape(bf16[12288,8,48]{2,1,0:T(8,128)(2,1)} %bitcast.81) | data formatting | bytes 18874368
  351.0 13.4 %reshape.141 = bf16[8192,8,16]{2,1,0:T(8,128)(2,1)} reshape(bf16[4,2,131072]{2,1,0:T(2,128)(2,1)S(1)} %all-to-all-done.1) | data formatting | bytes 4194304
  364.4 17.4 %copy.99 = bf16[8,16,4,2048]{3,2,1,0:T(4,128)(2,1)S(1)} copy(bf16[8,16,4,2048]{1,0,3,2:T(8,128)(2,1)} %bitcast.85) | data formatting | bytes 4194304 | tf_op jit(solution)/shard_map/all_to_all | solution.py:68
  385.1 14.3 %reshape.137 = bf16[8192,8,16]{2,1,0:T(8,128)(2,1)} reshape(bf16[4,2,131072]{2,1,0:T(2,128)(2,1)} %all-to-all-done.2) | data formatting | bytes 4194304
  399.4 17.4 %copy.104 = bf16[8,16,4,2048]{3,2,1,0:T(4,128)(2,1)S(1)} copy(bf16[8,16,4,2048]{1,0,3,2:T(8,128)(2,1)} %bitcast.86) | data formatting | bytes 4194304 | tf_op jit(solution)/shard_map/all_to_all | solution.py:69
  420.0 21.6 %all-to-all-done = bf16[4,2,589824]{2,1,0:T(2,128)(2,1)} async-done(((bf16[4,2,589824]{2,1,0:T(2,128)(2,1)}), bf16[4,2,589824]{2,1,0:T(2,128)(2,1)}, u32[]{:S(2)}, u32[]{:S(2)}) %all-to-all-start) | async-done | bytes 9437216 | tf_op jit(solution)/shard_map/all_to_all | solution.py:67
  441.6 40.7 %reshape.139 = bf16[12288,8,48]{2,1,0:T(8,128)(2,1)} reshape(bf16[4,2,589824]{2,1,0:T(2,128)(2,1)} %all-to-all-done) | data formatting | bytes 18874368
  482.3 28.1 %copy.98 = bf16[8,48,4,3072]{3,2,1,0:T(4,128)(2,1)} copy(bf16[8,48,4,3072]{1,0,3,2:T(8,128)(2,1)} %bitcast.82) | data formatting | bytes 18874368 | tf_op jit(solution)/shard_map/all_to_all | solution.py:67
  510.4 10.7 %copy.69 = bf16[8,4,48,3072]{3,2,1,0:T(8,128)(2,1)} copy(bf16[8,4,48,3072]{3,1,2,0:T(4,128)(2,1)} %bitcast.87) | data formatting | bytes 18874368 | tf_op jit(solution)/shard_map/all_to_all | solution.py:67
  553.2 23.9 %fusion.2 = f32[128,4,16,256]{3,2,1,0:T(8,128)} fusion(bf16[128,256,512]{2,1,0:T(8,128)(2,1)} %param.14, bf16[128,4,16,512]{3,0,1,2:T(8,128)(2,1)} %copy-done.3), kind=kOutput, calls=%fused_computation.2 | convolution fusion | flops 2147483648 | bytes 50331648 | tf_op jit(solution)/shard_map/sqhc,stc->sqht/dot_general | solution.py:104
  594.8 21.2 %fusion = f32[128,4,16,512]{3,2,1,0:T(8,128)} fusion(bf16[128,256,512]{2,1,0:T(8,128)(2,1)} %param.14, bf16[128,4,16,260]{3,2,1,0:T(8,128)(2,1)} %divide_convert_fusion), kind=kOutput, calls=%fused_computation | convolution fusion | flops 2147483648 | bytes 54525952 | tf_op jit(solution)/shard_map/sqht,stc->sqhc/dot_general | solution.py:126
  616.0 10.3 %add_convert_fusion = bf16[128,4,16,512]{3,2,1,0:T(8,128)(2,1)} fusion(f32[128,4,16,512]{3,2,1,0:T(8,128)} %fusion, bf16[128,4,16,260]{3,2,1,0:T(8,128)(2,1)} %divide_convert_fusion, bf16[128,4,512,1]{2,1,0,3:T(4,128)(2,1)S(1)} %copy-done.6), kind=kOutput, calls=%fused_computation.4 | convolution fusion | flops 41943040 | bytes 27787264 | tf_op jit(solution)/shard_map/sqhk,skc->sqhc/dot_general | solution.py:131
  626.3 13.6 %convert_bitcast_fusion.1 = bf16[128,4,16,128]{0,3,1,2:T(8,128)(2,1)S(1)} fusion(bf16[512,16,128,1]{2,1,0,3:T(8,128)(2,1)S(1)} %bitcast.102, bf16[128,4,16,512]{3,2,1,0:T(8,128)(2,1)} %add_convert_fusion), kind=kOutput, calls=%fused_computation.34 | convolution fusion | flops 1074790400 | bytes 12582912 | tf_op jit(solution)/shard_map/sqhc,chv->sqhv/dot_general | solution.py:135
  643.7 165.2 %all-gather.8.cloned.1.call-done = bf16[2048,7168]{0,1:T(8,128)(2,1)} async-done(((bf16[2048,896]{0,1:T(8,128)(2,1)}), bf16[2048,7168]{0,1:T(8,128)(2,1)}) %all-gather.8.cloned.1.call-update) | async-done | bytes 29360144 | tf_op jit(solution)/shard_map/all_gather | solution.py:148
  809.0 23.8 %fusion.36 = f32[512,7168]{1,0:T(8,128)} fusion(bf16[512,2048]{1,0:T(8,128)(2,1)} %reshape.123, bf16[2048,7168]{0,1:T(8,128)(2,1)} %all-gather.8.cloned.1.call-done), kind=kOutput, calls=%fused_computation.56 | convolution fusion | flops 15032385536 | bytes 46137344 | tf_op jit(solution)/shard_map/dot_general | solution.py:146
  835.3 39.9 %psum.7 = f32[]{:T(128)} all-reduce(f32[]{:T(128)S(6)} %add.51), channel_id=1, replica_groups=mesh['dp'=8,'tp'=4] {'dp','tp'}, use_global_device_ids=true, to_apply=%region_8.9 | all-reduce | flops 1 | bytes 8 | tf_op jit(solution)/shard_map/psum | solution.py:54
  875.9 67.7 %reduce-scatter.2.cloned.1.call-done = f32[512,1792]{1,0:T(8,128)} async-done(((f32[512,7168]{1,0:T(8,128)}), f32[512,1792]{1,0:T(8,128)}) %reduce-scatter.2.cloned.1.call-update) | async-done | bytes 3670032 | tf_op jit(solution)/shard_map/reduce_scatter | solution.py:151
  (86 shorter events, 110.6 us)
Async XLA Ops:
  7.2 339.5 %copy-start = (bf16[128,4,64]{0,2,1:T(8,128)(2,1)S(1)}, bf16[128,4,64]{0,2,1:T(8,128)(2,1)}, u32[]{:S(2)}) copy-start(bf16[128,4,64]{0,2,1:T(8,128)(2,1)} %param.13) | copy-start | bytes 196612
  7.2 65.1 %all-gather.12.cloned.1.call-start = ((), (), s32[]{:S(2)}) async-start(), calls=%async_computation.8 | async-start | bytes 2359296 | tf_op jit(solution)/shard_map/all_gather | solution.py:63
  9.8 102.0 %all-gather.14.cloned.1.call-start = ((), (), s32[]{:S(2)}) async-start(), calls=%async_computation.9 | async-start | bytes 2359296 | tf_op jit(solution)/shard_map/all_gather | solution.py:64
  12.5 237.9 %all-gather.10.cloned.1.call-start = ((), (), s32[]{:S(2)}) async-start(), calls=%async_computation.7 | async-start | bytes 10616832 | tf_op jit(solution)/shard_map/all_gather | solution.py:62
  17.1 791.9 %all-gather.8.cloned.1.call-start = ((), (), s32[]{:S(2)}) async-start(), calls=%async_computation.5 | async-start | bytes 33030144 | tf_op jit(solution)/shard_map/all_gather | solution.py:148
  107.1 39.5 %all-to-all-start.1 = ((bf16[4,2,131072]{2,1,0:T(2,128)(2,1)}), bf16[4,2,131072]{2,1,0:T(2,128)(2,1)S(1)}, u32[]{:S(2)}, u32[]{:S(2)}) async-start(bf16[4,2,131072]{2,1,0:T(2,128)(2,1)} %reshape.140), calls=%async_computation.1 | async-start | bytes 4194304 | tf_op jit(solution)/shard_map/all_to_all | solution.py:68
  146.6 184.7 %all-to-all-start.2 = ((bf16[4,2,131072]{2,1,0:T(2,128)(2,1)}), bf16[4,2,131072]{2,1,0:T(2,128)(2,1)}, u32[]{:S(2)}, u32[]{:S(2)}) async-start(bf16[4,2,131072]{2,1,0:T(2,128)(2,1)} %reshape.136), calls=%async_computation.2 | async-start | bytes 4194304 | tf_op jit(solution)/shard_map/all_to_all | solution.py:69
  331.3 7.8 copy-start.11
  331.3 110.3 %all-to-all-start = ((bf16[4,2,589824]{2,1,0:T(2,128)(2,1)}), bf16[4,2,589824]{2,1,0:T(2,128)(2,1)}, u32[]{:S(2)}, u32[]{:S(2)}) async-start(bf16[4,2,589824]{2,1,0:T(2,128)(2,1)} %reshape.138), calls=%async_computation | async-start | bytes 18874368 | tf_op jit(solution)/shard_map/all_to_all | solution.py:67
  337.2 606.4 %reduce-scatter.2.cloned.1.call-start = ((), (), s32[]{:S(2)}) async-start(), calls=%async_computation.6 | async-start | bytes 18350080 | tf_op jit(solution)/shard_map/reduce_scatter | solution.py:151
  337.3 7.7 copy-start.10
  339.1 8.8 copy-start.12
  534.8 1.6 slice-start.1
  536.4 0.9 copy-start.8
  537.3 2.0 slice-start
  537.3 2.2 copy-start.5
  539.3 9.9 %copy-start.4 = (bf16[128,4,16,32]{3,2,1,0:T(8,128)(2,1)}, bf16[128,4,16,32]{3,2,1,0:T(8,128)(2,1)S(1)}, u32[]{:S(2)}) copy-start(bf16[128,4,16,32]{3,2,1,0:T(8,128)(2,1)S(1)} %get-tuple-element.5) | copy-start | bytes 1572868
  539.5 4.8 copy-start.6
  544.4 4.8 copy-start.3
  544.4 4.8 copy-start.9
  577.0 8.9 copy-start.2
  616.0 10.4 %copy-start.7 = (bf16[64,8,16,128]{3,2,1,0:T(8,128)(2,1)S(1)}, bf16[64,8,16,128]{3,2,1,0:T(8,128)(2,1)}, u32[]{:S(2)}) copy-start(bf16[64,8,16,128]{3,2,1,0:T(8,128)(2,1)} %copy.112) | copy-start | bytes 6291460
  875.9 71.5 %copy-start.1 = (bf16[128,4,64]{0,2,1:T(8,128)(2,1)S(1)}, bf16[128,4,64]{0,2,1:T(8,128)(2,1)}, u32[]{:S(2)}) copy-start(bf16[128,4,64]{0,2,1:T(8,128)(2,1)} %param.13) | copy-start | bytes 196612
Sparse Core Ops, SparseCore 0:
  10.1 51.7 all-gather.11
  64.1 47.6 all-gather.13
  114.5 135.7 all-gather.9
  251.7 557.1 all-gather.7
  832.9 110.7 reduce-scatter.1
where the time goes:
time: 965 us; the launch traced here: 955 us
  waiting for transfers between devices  355 us (37%)
  local copies, waits for them, and re-layouts  320 us (33%)
  matrix products  126 us (13%)
  blocking collectives  86.6 us (9%)
  other arithmetic  34.3 us (4%)
  between operations  18.9 us (2%)
  starting transfers between devices  14.4 us (1%)
    unnamed x36, local copies, waits for them, and re-layouts  171 us
    all_gather x1, waiting for transfers between devices, shards(): lax.all_gather(out_rows, 'dp', axis=1, tiled=True)  165 us
    all_gather x1, waiting for transfers between devices, shards(): lax.all_gather(query_cast[None], 'dp', axis=0, tiled=True)  99.3 us
    reduce_scatter x1, waiting for transfers between devices, shards(): lax.psum_scatter(partial_out, 'tp', scatter_dimension=1, tiled=True)  67.7 us
    all_to_all x1, blocking collectives, shards(): lax.all_to_all(out_cast, 'tp', split_axis=0, concat_axis=1, tiled=True)  46.7 us
    psum x1, blocking collectives, shards(): squares_total = lax.psum(local_squares, ('dp', 'tp'))  39.9 us
    all_to_all x2, local copies, waits for them, and re-layouts, shards(): lax.all_to_all(gathered[0], 'tp', split_axis=2, concat_axis=1, tiled=True)  38.7 us
    all_gather x1, local copies, waits for them, and re-layouts, shards(): lax.all_gather(query_cast[None], 'dp', axis=0, tiled=True)  26.1 us
  transfers between devices with their start and end apart: 8, of which 5 were waited for; matrix products, arithmetic and copies ran while one was open for 47% of the time, Pallas kernels for 0%

commit v1 on v0

--- a/solution.py
+++ b/solution.py
@@ -1,3 +1,4 @@
+import functools
 import jax
 import jax.numpy as jnp
 from jax import lax
@@ -12,6 +13,16 @@
 HEADS = 64
 NEWTOK = 4
 CACHE = 256
+
+
+def samples_work(page, where_dim):
+    next_value = jnp.concatenate(
+        lax.all_to_all(jnp.stack([page] * lax.axis_size("dp"), 0), "dp", 0, 0), where_dim
+    )
+    return next_value
+
+
+samples_check = functools.partial(samples_work, where_dim=0)
 
 
 def widen(values):
@@ -59,7 +70,7 @@
     key_cast = w_uk.astype(jnp.bfloat16)
     value_cast = w_uv.astype(jnp.bfloat16)
     gathered = (
-        lax.all_gather(query_cast[None], "dp", axis=0, tiled=True),
+        samples_check(query_cast[None]),
         lax.all_gather(key_cast[None], "dp", axis=0, tiled=True),
         lax.all_gather(value_cast[None], "dp", axis=0, tiled=True),
     )

time: 965 us -> 1050 us (1.088)
  blocking collectives: 86.6 us -> 154 us
  waiting for transfers between devices: 355 us -> 366 us
    all_to_all x0 -> x1, waiting for transfers between devices: none -> 255 us  [samples_work(): lax.all_to_all(jnp.stack([page] * lax.axis_size('dp'), 0), 'dp', 0, 0)]
    all_gather x1, waiting for transfers between devices: 165 us -> 0.01 us  [shards(): lax.all_gather(out_rows, 'dp', axis=1, tiled=True)]
    all_gather x1 -> x0, waiting for transfers between devices: 99.3 us -> none  [shards(): lax.all_gather(query_cast[None], 'dp', axis=0, tiled=True)]
    psum x1, blocking collectives: 39.9 us -> 107 us  [shards(): squares_total = lax.psum(local_squares, ('dp', 'tp'))]
    all_gather x1 -> x0, local copies, waits for them, and re-layouts: 26.1 us -> none  [shards(): lax.all_gather(query_cast[None], 'dp', axis=0, tiled=True)]
    reshape x0 -> x1, local copies, waits for them, and re-layouts: none -> 26.1 us  [samples_work(): jnp.concatenate(lax.all_to_all(jnp.stack([page] * lax.axis_size('dp'), 0)...]
    all_to_all x1, waiting for transfers between devices: 0.01 us -> 22 us  [shards(): lax.all_to_all(gathered[1], 'tp', split_axis=2, concat_axis=1, tiled=True)]
  transfers between devices with their start and end apart: 8 -> 8, of which waited for: 5 -> 4; matrix products, arithmetic and copies ran while one was open for 47% -> 43% of each run, Pallas kernels for 0% -> 0%
where the time goes in v1:
time: 1050 us; the launch traced here: 1040 us
  waiting for transfers between devices  366 us (35%)
  local copies, waits for them, and re-layouts  325 us (31%)
  blocking collectives  154 us (15%)
  matrix products  126 us (12%)
  other arithmetic  33.2 us (3%)
  starting transfers between devices  20.9 us (2%)
  between operations  18.8 us (2%)
    all_to_all x1, waiting for transfers between devices, samples_work(): lax.all_to_all(jnp.stack([page] * lax.axis_size('dp'), 0), 'dp', 0, 0)  255 us
    unnamed x36, local copies, waits for them, and re-layouts  171 us
    psum x1, blocking collectives, shards(): squares_total = lax.psum(local_squares, ('dp', 'tp'))  107 us
    reduce_scatter x1, waiting for transfers between devices, shards(): lax.psum_scatter(partial_out, 'tp', scatter_dimension=1, tiled=True)  67.6 us
    all_to_all x1, blocking collectives, shards(): lax.all_to_all(out_cast, 'tp', split_axis=0, concat_axis=1, tiled=True)  46.7 us
    all_to_all x2, local copies, waits for them, and re-layouts, shards(): lax.all_to_all(gathered[0], 'tp', split_axis=2, concat_axis=1, tiled=True)  38.7 us
    reshape x1, local copies, waits for them, and re-layouts, samples_work(): jnp.concatenate(lax.all_to_all(jnp.stack([page] * lax.axis_size('dp'), 0)...  26.1 us
    dot_general x1, matrix products, shards(): jnp.dot(request_out, lax.all_gather(out_rows, 'dp', axis=1, tiled=True),...  23.8 us
  transfers between devices with their start and end apart: 8, of which 4 were waited for; matrix products, arithmetic and copies ran while one was open for 43% of the time, Pallas kernels for 0%

profile of v1, /device:TPU:0, one launch (start us, length us, event | category | flops | bytes accessed | tf_op | source)
XLA Modules:
  0.0 1043.4 jit_solution(10515301430527426883)
XLA Ops:
  20.6 46.7 %all_to_all.69 = bf16[4,2048,224]{1,2,0:T(8,128)(2,1)} all-to-all(bf16[4,2048,224]{1,2,0:T(8,128)(2,1)S(1)} %bitcast.89), channel_id=1, replica_groups=mesh['dp'=8,'tp'=4] {'tp'}, dimensions={0} | all-to-all | bytes 7340032 | tf_op jit(solution)/shard_map/all_to_all | solution.py:156
  67.4 14.5 %copy.71 = bf16[8,16,8192]{1,0,2:T(8,128)(2,1)} copy(bf16[8,16,8192]{2,1,0:T(8,128)(2,1)} %bitcast.100) | data formatting | bytes 4194304 | tf_op jit(solution)/shard_map/all_gather | solution.py:74
  81.8 20.4 %reshape.145 = bf16[4,2,131072]{2,1,0:T(2,128)(2,1)} reshape(bf16[8192,8,16]{2,1,0:T(8,128)(2,1)} %bitcast.83) | data formatting | bytes 4194304
  109.4 22.0 %all-to-all-done.2 = bf16[4,2,131072]{2,1,0:T(2,128)(2,1)S(1)} async-done(((bf16[4,2,131072]{2,1,0:T(2,128)(2,1)}), bf16[4,2,131072]{2,1,0:T(2,128)(2,1)S(1)}, u32[]{:S(2)}, u32[]{:S(2)}) %all-to-all-start.2) | async-done | bytes 2097184 | tf_op jit(solution)/shard_map/all_to_all | solution.py:79
  143.0 14.4 %copy.82 = bf16[8,16,8192]{1,0,2:T(8,128)(2,1)} copy(bf16[8,16,8192]{2,1,0:T(8,128)(2,1)} %bitcast.99) | data formatting | bytes 4194304 | tf_op jit(solution)/shard_map/all_gather | solution.py:75
  157.4 20.3 %reshape.141 = bf16[4,2,131072]{2,1,0:T(2,128)(2,1)} reshape(bf16[8192,8,16]{2,1,0:T(8,128)(2,1)} %bitcast.84) | data formatting | bytes 4194304
  177.8 255.0 %all-to-all-done = bf16[8,1,48,12288]{3,2,1,0:T(8,128)(2,1)} async-done(((bf16[8,1,48,12288]{3,2,1,0:T(8,128)(2,1)}), bf16[8,1,48,12288]{3,2,1,0:T(8,128)(2,1)}, u32[]{:S(2)}, u32[]{:S(2)}) %all-to-all-start) | async-done | bytes 9437216 | tf_op jit(solution)/shard_map/all_to_all | solution.py:20
  437.2 26.1 %copy.67 = bf16[8,48,12288]{1,0,2:T(8,128)(2,1)} copy(bf16[8,48,12288]{2,1,0:T(8,128)(2,1)} %bitcast.1) | data formatting | bytes 18874368 | tf_op jit(solution)/shard_map/reshape | solution.py:19
  463.3 54.9 %reshape.143 = bf16[4,2,589824]{2,1,0:T(2,128)(2,1)} reshape(bf16[12288,8,48]{2,1,0:T(8,128)(2,1)} %bitcast.81) | data formatting | bytes 18874368
  538.0 13.5 %reshape.146 = bf16[8192,8,16]{2,1,0:T(8,128)(2,1)} reshape(bf16[4,2,131072]{2,1,0:T(2,128)(2,1)S(1)} %all-to-all-done.2) | data formatting | bytes 4194304
  551.4 17.4 %copy.99 = bf16[8,16,4,2048]{3,2,1,0:T(4,128)(2,1)S(1)} copy(bf16[8,16,4,2048]{1,0,3,2:T(8,128)(2,1)} %bitcast.85) | data formatting | bytes 4194304 | tf_op jit(solution)/shard_map/all_to_all | solution.py:79
  572.1 14.4 %reshape.142 = bf16[8192,8,16]{2,1,0:T(8,128)(2,1)} reshape(bf16[4,2,131072]{2,1,0:T(2,128)(2,1)} %all-to-all-done.3) | data formatting | bytes 4194304
  586.4 17.4 %copy.104 = bf16[8,16,4,2048]{3,2,1,0:T(4,128)(2,1)S(1)} copy(bf16[8,16,4,2048]{1,0,3,2:T(8,128)(2,1)} %bitcast.86) | data formatting | bytes 4194304 | tf_op jit(solution)/shard_map/all_to_all | solution.py:80
  607.0 21.6 %all-to-all-done.1 = bf16[4,2,589824]{2,1,0:T(2,128)(2,1)} async-done(((bf16[4,2,589824]{2,1,0:T(2,128)(2,1)}), bf16[4,2,589824]{2,1,0:T(2,128)(2,1)}, u32[]{:S(2)}, u32[]{:S(2)}) %all-to-all-start.1) | async-done | bytes 9437216 | tf_op jit(solution)/shard_map/all_to_all | solution.py:78
  628.6 40.7 %reshape.144 = bf16[12288,8,48]{2,1,0:T(8,128)(2,1)} reshape(bf16[4,2,589824]{2,1,0:T(2,128)(2,1)} %all-to-all-done.1) | data formatting | bytes 18874368
  669.3 28.0 %copy.98 = bf16[8,48,4,3072]{3,2,1,0:T(4,128)(2,1)} copy(bf16[8,48,4,3072]{1,0,3,2:T(8,128)(2,1)} %bitcast.82) | data formatting | bytes 18874368 | tf_op jit(solution)/shard_map/all_to_all | solution.py:78
  697.3 10.7 %copy.69 = bf16[8,4,48,3072]{3,2,1,0:T(8,128)(2,1)} copy(bf16[8,4,48,3072]{3,1,2,0:T(4,128)(2,1)} %bitcast.87) | data formatting | bytes 18874368 | tf_op jit(solution)/shard_map/all_to_all | solution.py:78
  740.1 23.1 %fusion.2 = f32[128,4,16,256]{3,2,1,0:T(8,128)} fusion(bf16[128,256,512]{2,1,0:T(8,128)(2,1)} %param.14, bf16[128,4,16,512]{3,0,1,2:T(8,128)(2,1)} %copy-done.3), kind=kOutput, calls=%fused_computation.2 | convolution fusion | flops 2147483648 | bytes 50331648 | tf_op jit(solution)/shard_map/sqhc,stc->sqht/dot_general | solution.py:115
  781.0 21.0 %fusion = f32[128,4,16,512]{3,2,1,0:T(8,128)} fusion(bf16[128,256,512]{2,1,0:T(8,128)(2,1)} %param.14, bf16[128,4,16,260]{3,2,1,0:T(8,128)(2,1)} %divide_convert_fusion), kind=kOutput, calls=%fused_computation | convolution fusion | flops 2147483648 | bytes 54525952 | tf_op jit(solution)/shard_map/sqht,stc->sqhc/dot_general | solution.py:137
  802.1 10.4 add_convert_fusion
  812.4 13.6 %convert_bitcast_fusion.1 = bf16[128,4,16,128]{0,3,1,2:T(8,128)(2,1)S(1)} fusion(bf16[512,16,128,1]{2,1,0,3:T(8,128)(2,1)S(1)} %bitcast.101, bf16[128,4,16,512]{3,2,1,0:T(8,128)(2,1)} %add_convert_fusion), kind=kOutput, calls=%fused_computation.34 | convolution fusion | flops 1074790400 | bytes 12582912 | tf_op jit(solution)/shard_map/sqhc,chv->sqhv/dot_general | solution.py:146
  829.8 23.8 %fusion.36 = f32[512,7168]{1,0:T(8,128)} fusion(bf16[512,2048]{1,0:T(8,128)(2,1)} %reshape.129, bf16[2048,7168]{0,1:T(8,128)(2,1)} %all-gather.6.cloned.1.call-done), kind=kOutput, calls=%fused_computation.56 | convolution fusion | flops 15032385536 | bytes 46137344 | tf_op jit(solution)/shard_map/dot_general | solution.py:157
  856.0 107.3 %psum.7 = f32[]{:T(128)} all-reduce(f32[]{:T(128)S(6)} %add.51), channel_id=1, replica_groups=mesh['dp'=8,'tp'=4] {'dp','tp'}, use_global_device_ids=true, to_apply=%region_8.9 | all-reduce | flops 1 | bytes 8 | tf_op jit(solution)/shard_map/psum | solution.py:65
  964.0 67.6 %reduce-scatter.2.cloned.1.call-done = f32[512,1792]{1,0:T(8,128)} async-done(((f32[512,7168]{1,0:T(8,128)}), f32[512,1792]{1,0:T(8,128)}) %reduce-scatter.2.cloned.1.call-update) | async-done | bytes 3670032 | tf_op jit(solution)/shard_map/reduce_scatter | solution.py:162
  (86 shorter events, 119.9 us)
Async XLA Ops:
  7.2 526.5 %copy-start = (bf16[128,4,64]{0,2,1:T(8,128)(2,1)S(1)}, bf16[128,4,64]{0,2,1:T(8,128)(2,1)}, u32[]{:S(2)}) copy-start(bf16[128,4,64]{0,2,1:T(8,128)(2,1)} %param.13) | copy-start | bytes 196612
  7.2 60.2 %all-gather.8.cloned.1.call-start = ((), (), s32[]{:S(2)}) async-start(), calls=%async_computation.8 | async-start | bytes 2359296 | tf_op jit(solution)/shard_map/all_gather | solution.py:74
  9.8 133.2 %all-gather.10.cloned.1.call-start = ((), (), s32[]{:S(2)}) async-start(), calls=%async_computation.9 | async-start | bytes 2359296 | tf_op jit(solution)/shard_map/all_gather | solution.py:75
  12.5 817.3 %all-gather.6.cloned.1.call-start = ((), (), s32[]{:S(2)}) async-start(), calls=%async_computation.6 | async-start | bytes 33030144 | tf_op jit(solution)/shard_map/all_gather | solution.py:159
  102.2 29.3 %all-to-all-start.2 = ((bf16[4,2,131072]{2,1,0:T(2,128)(2,1)}), bf16[4,2,131072]{2,1,0:T(2,128)(2,1)S(1)}, u32[]{:S(2)}, u32[]{:S(2)}) async-start(bf16[4,2,131072]{2,1,0:T(2,128)(2,1)} %reshape.145), calls=%async_computation.2 | async-start | bytes 4194304 | tf_op jit(solution)/shard_map/all_to_all | solution.py:79
  136.2 296.6 %all-to-all-start = ((bf16[8,1,48,12288]{3,2,1,0:T(8,128)(2,1)}), bf16[8,1,48,12288]{3,2,1,0:T(8,128)(2,1)}, u32[]{:S(2)}, u32[]{:S(2)}) async-start(bf16[8,1,48,12288]{3,2,1,0:T(8,128)(2,1)} %stack.3), calls=%async_computation | async-start | bytes 18874368 | tf_op jit(solution)/shard_map/all_to_all | solution.py:20
  432.8 85.5 %all-to-all-start.3 = ((bf16[4,2,131072]{2,1,0:T(2,128)(2,1)}), bf16[4,2,131072]{2,1,0:T(2,128)(2,1)}, u32[]{:S(2)}, u32[]{:S(2)}) async-start(bf16[4,2,131072]{2,1,0:T(2,128)(2,1)} %reshape.141), calls=%async_computation.3 | async-start | bytes 4194304 | tf_op jit(solution)/shard_map/all_to_all | solution.py:80
  518.3 7.8 copy-start.11
  518.3 110.3 %all-to-all-start.1 = ((bf16[4,2,589824]{2,1,0:T(2,128)(2,1)}), bf16[4,2,589824]{2,1,0:T(2,128)(2,1)}, u32[]{:S(2)}, u32[]{:S(2)}) async-start(bf16[4,2,589824]{2,1,0:T(2,128)(2,1)} %reshape.143), calls=%async_computation.1 | async-start | bytes 18874368 | tf_op jit(solution)/shard_map/all_to_all | solution.py:78
  524.2 507.5 %reduce-scatter.2.cloned.1.call-start = ((), (), s32[]{:S(2)}) async-start(), calls=%async_computation.7 | async-start | bytes 18350080 | tf_op jit(solution)/shard_map/reduce_scatter | solution.py:162
  524.2 7.7 copy-start.10
  526.0 8.8 copy-start.12
  721.7 1.6 slice-start.1
  723.3 0.9 copy-start.8
  724.2 2.0 slice-start
  724.2 2.2 copy-start.5
  726.2 9.9 copy-start.4
  726.5 4.8 copy-start.6
  731.3 4.8 copy-start.3
  731.3 4.8 copy-start.9
  763.2 8.9 copy-start.2
  802.1 10.4 copy-start.7
  964.0 71.3 %copy-start.1 = (bf16[128,4,64]{0,2,1:T(8,128)(2,1)S(1)}, bf16[128,4,64]{0,2,1:T(8,128)(2,1)}, u32[]{:S(2)}) copy-start(bf16[128,4,64]{0,2,1:T(8,128)(2,1)} %param.13) | copy-start | bytes 196612
Sparse Core Ops, SparseCore 0:
  10.1 51.8 all-gather.7
  64.7 47.6 all-gather.9
  114.0 665.0 all-gather.5
  853.7 177.9 reduce-scatter.1
